TPU v7x, 256 devices: a whole 4x4x8 slice. The times are simulated.
256 devices in a mesh: bank: 16 (over z, core), zero: 16 (over y, x).
Axes of the slice: x: 4, y: 4, z: 8, core: 2. Of those that a mesh axis runs over, the one named last changes fastest.
Arguments:
- master_gate: float32 [64, 2048, 1408], P('bank', 'zero'), may hold values from -0.1875 to 0.1875
- master_up: float32 [64, 2048, 1408], P('bank', 'zero'), may hold values from -0.1875 to 0.1875
- master_down: float32 [64, 1408, 2048], P('bank', None, 'zero'), may hold values from -0.21875 to 0.21875
- router_weight: float32 [2048, 64], P('zero', 'bank'), may hold values from -0.125 to 0.125
- router_gain: float32 [2048], P('zero'), may hold values from 0.25 to 1.75
Outputs:
- final_gate: bfloat16 [64, 2048, 1408], P('bank', None, 'zero')
- final_up: bfloat16 [64, 2048, 1408], P('bank', None, 'zero')
- final_down: bfloat16 [64, 1408, 2048], P('bank', 'zero')
- scale_gate: float32 [64, 1408], P('bank', 'zero')
- scale_up: float32 [64, 1408], P('bank', 'zero')
- scale_down: float32 [64, 1408], P('bank', 'zero')
- serve_router: bfloat16 [2048, 64], replicated
All inputs are finite; a program needn't handle non-finite values. Where the computation divides by a largest or mean magnitude, that divisor is 1e-20 or more.
Results may differ from a plain program's by a relative error of at most 0.0013.
Values may be sent and summed in bfloat16 or wider, within the bound.
No kernel may reach another device: no remote copies, remote signals or barrier semaphores. Data moves between devices by JAX's collectives and lax.ppermute only.
A program may use at most 64 MiB of HBM per device.

v0:
```python
import jax
import jax.numpy as jnp
from jax import lax
from jax.sharding import PartitionSpec as P

D_MODEL = 2048


def copy_for_each(x, axis):
    count = lax.axis_size(axis)
    return lax.all_to_all(jnp.broadcast_to(x[None], (count, *x.shape)), axis, 0, 0, tiled=True)


def taken_together(x, axis):
    return copy_for_each(x, axis).sum(axis=0)


def in_one(arrays, axis):
    vector, at, finished = (jnp.concatenate([a.reshape(-1) for a in arrays]), 0, [])
    total = taken_together(vector, axis)
    for a in arrays:
        finished.append(total[at : at + a.size].reshape(a.shape))
        at += a.size
    return tuple(finished)


def side_by_side(arrays, axis, split_dim, concat_dim, along):
    both = jnp.concatenate(arrays, axis=along)
    whole, at, finished = (
        lax.all_to_all(both, axis, split_axis=split_dim, concat_axis=concat_dim, tiled=True),
        0,
        [],
    )
    for a in arrays:
        finished.append(lax.slice_in_dim(whole, at, at + a.shape[along], axis=along))
        at += a.shape[along]
    return tuple(finished)


def laid_out(pieces, dim):
    shape = list(pieces.shape[1:])
    shape[dim] *= pieces.shape[0]
    return jnp.moveaxis(pieces, 0, dim).reshape(shape)


def gather_directly(x, axis, dim):
    pieces = copy_for_each(x, axis)
    return laid_out(pieces, dim)


def local(master_gate, master_up, master_down, router_weight, router_gain):
    total_gate, total_up, total_down = in_one(
        (
            jnp.sum(jnp.abs(master_gate), axis=1),
            jnp.sum(jnp.abs(master_up), axis=1),
            jnp.sum(jnp.abs(master_down), axis=2),
        ),
        "zero",
    )
    scale_gate = total_gate / D_MODEL
    scale_up = total_up / D_MODEL
    scale_down = total_down / D_MODEL
    narrow_gate, narrow_up, narrow_down = (
        (master_gate / jnp.expand_dims(scale_gate, 1)).astype(jnp.bfloat16),
        (master_up / jnp.expand_dims(scale_up, 1)).astype(jnp.bfloat16),
        (master_down / jnp.expand_dims(scale_down, 2)).astype(jnp.bfloat16),
    )
    final_gate, final_up = side_by_side((narrow_gate, narrow_up), "zero", 2, 1, 0)
    final_down = lax.all_to_all(narrow_down, "zero", split_axis=1, concat_axis=2, tiled=True)
    scale_gate = lax.dynamic_slice_in_dim(
        scale_gate, lax.axis_index("zero") * final_gate.shape[2], final_gate.shape[2], axis=1
    )
    scale_up = lax.dynamic_slice_in_dim(
        scale_up, lax.axis_index("zero") * final_up.shape[2], final_up.shape[2], axis=1
    )
    scale_down = lax.dynamic_slice_in_dim(
        scale_down, lax.axis_index("zero") * final_down.shape[1], final_down.shape[1], axis=1
    )
    part_router = (router_weight * router_gain[:, None]).astype(jnp.bfloat16)
    row_router = gather_directly(part_router, "zero", 0)
    serve_router = lax.all_gather(row_router, "bank", axis=1, tiled=True)
    return (final_gate, final_up, final_down, scale_gate, scale_up, scale_down, serve_router)


def solution(mesh):
    placed = (
        P("bank", "zero", None),
        P("bank", "zero", None),
        P("bank", None, "zero"),
        P("zero", "bank"),
        P("zero"),
    )
    return jax.shard_map(
        local,
        mesh=mesh,
        in_specs=placed,
        out_specs=(
            P("bank", None, "zero"),
            P("bank", None, "zero"),
            P("bank", "zero", None),
            P("bank", "zero"),
            P("bank", "zero"),
            P("bank", "zero"),
            P(),
        ),
        check_vma=False,
    )
```

profile of v0, /device:TPU:224, one launch (start us, length us, event | category | flops | bytes accessed | tf_op | source)
XLA Modules:
  0.0 125.6 jit_solution(8950060846199024515)
XLA Ops:
  0.6 2.2 %abs_reduce_fusion.2 = f32[4,1408]{1,0:T(4,128)S(1)} fusion(f32[4,128,1408]{2,1,0:T(8,128)} %param.5), kind=kLoop, calls=%fused_computation.4 | loop fusion | flops 1436160 | bytes 2906112 | tf_op jit(solution)/shard_map/reduce_sum | solution.py:54
  2.9 0.4 copy-done.1
  3.3 0.2 abs_reduce_fusion.1
  3.6 2.8 %abs_reduce_fusion = f32[4,1408]{1,0:T(4,128)S(1)} fusion(f32[4,1408,128]{2,1,0:T(8,128)} %param.7), kind=kLoop, calls=%fused_computation.2 | loop fusion | flops 1436160 | bytes 2906112 | tf_op jit(solution)/shard_map/reduce_sum | solution.py:56
  6.4 1.5 %broadcast_in_dim.4 = f32[16,1,16896]{2,1,0:T(1,128)} broadcast(f32[16896]{0:T(1024)S(1)} %pad_maximum_fusion.1), dimensions={2} | broadcast | bytes 1148928 | tf_op jit(solution)/shard_map/broadcast_in_dim | solution.py:11
  8.0 7.1 %all-to-all-start = ((f32[16,1,16896]{2,1,0:T(1,128)}), f32[16,1,16896]{2,1,0:T(1,128)}, u32[]{:S(2)}, u32[]{:S(2)}) async-start(f32[16,1,16896]{2,1,0:T(1,128)} %broadcast_in_dim.4), calls=%async_computation | async-start | bytes 2162688 | tf_op jit(solution)/shard_map/all_to_all | solution.py:11
  15.1 2.9 %copy.44 = f32[4,128,1408]{1,0,2:T(4,128)} copy(f32[4,128,1408]{2,1,0:T(8,128)S(1)} %copy-done) | data formatting | bytes 5767168 | tf_op args[0]
  17.9 4.6 %copy.46 = f32[4,128,1408]{1,0,2:T(4,128)} copy(f32[4,128,1408]{2,1,0:T(8,128)} %param.6) | data formatting | bytes 5767168 | tf_op args[1]
  22.6 10.6 %all-to-all-done = f32[16,1,16896]{2,1,0:T(1,128)} async-done(((f32[16,1,16896]{2,1,0:T(1,128)}), f32[16,1,16896]{2,1,0:T(1,128)}, u32[]{:S(2)}, u32[]{:S(2)}) %all-to-all-start) | async-done | bytes 1081376 | tf_op jit(solution)/shard_map/all_to_all | solution.py:11
  33.2 0.6 broadcast_in_dim.5
  33.8 3.5 %all-to-all-start.3 = ((bf16[16,128,4]{1,2,0:T(4,128)(2,1)}), bf16[16,128,4]{1,2,0:T(4,128)(2,1)S(1)}, u32[]{:S(2)}, u32[]{:S(2)}) async-start(bf16[16,128,4]{1,2,0:T(4,128)(2,1)} %broadcast_in_dim.5), calls=%async_computation.3 | async-start | bytes 32768 | tf_op jit(solution)/shard_map/all_to_all | solution.py:11
  37.3 1.9 %reduce_sum.39 = f32[16896]{0:T(1024)S(1)} reduce(f32[16,1,16896]{2,1,0:T(1,128)} %all-to-all-done, f32[]{:T(128)} %constant.6.clone.1), dimensions={0,1}, to_apply=%region_3.0 | reduce | flops 253440 | bytes 1148932 | tf_op jit(solution)/shard_map/reduce_sum | solution.py:15
  39.2 1.2 copy.50
  40.4 7.7 %fusion = bf16[4,1408,128]{2,0,1:T(4,128)(2,1)} fusion(f32[4,1408,128]{2,1,0:T(8,128)S(1)} %copy-done.2, f32[4,1408]{0,1:T(8,128)} %copy.50), kind=kLoop, calls=%fused_computation.5 | loop fusion | flops 1441792 | bytes 4347904 | tf_op jit(solution)/shard_map/convert_element_type | solution.py:66
  48.1 1.2 copy.43
  49.3 1.2 copy.45
  50.5 7.2 %all-to-all-start.2 = ((bf16[4,1408,128]{2,0,1:T(4,128)(2,1)}), bf16[4,1408,128]{2,0,1:T(4,128)(2,1)}, u32[]{:S(2)}, u32[]{:S(2)}) async-start(bf16[4,1408,128]{2,0,1:T(4,128)(2,1)} %fusion), calls=%async_computation.2 | async-start | bytes 2883584 | tf_op jit(solution)/shard_map/all_to_all | solution.py:69
  57.7 6.6 %divide_convert_fusion = (bf16[4,128,1408]{1,0,2:T(4,128)(2,1)S(1)}, bf16[4,128,1408]{1,0,2:T(4,128)(2,1)S(1)}) fusion(f32[4,128,1408]{1,0,2:T(4,128)} %copy.46, f32[4,1408]{0,1:T(8,128)} %copy.45, f32[4,128,1408]{1,0,2:T(4,128)S(1)} %copy-done.3, f32[4,1408]{0,1:T(8,128)} %copy.43), kind=kLoop, calls=%fused_computation.6 | loop fusion | flops 2883584 | bytes 8695808 | tf_op jit(solution)/shard_map/convert_element_type | solution.py:65
  64.2 2.6 %pad_maximum_fusion = bf16[8,128,1408]{1,0,2:T(8,128)(2,1)} fusion(bf16[4,128,1408]{1,0,2:T(4,128)(2,1)S(1)} %get-tuple-element.12, bf16[4,128,1408]{1,0,2:T(4,128)(2,1)S(1)} %get-tuple-element.13), kind=kLoop, calls=%fused_computation | loop fusion | flops 5767168 | bytes 5767168 | tf_op jit(solution)/shard_map/concatenate | solution.py:28
  66.9 12.0 %all-to-all-done.2 = bf16[4,1408,128]{2,0,1:T(4,128)(2,1)} async-done(((bf16[4,1408,128]{2,0,1:T(4,128)(2,1)}), bf16[4,1408,128]{2,0,1:T(4,128)(2,1)}, u32[]{:S(2)}, u32[]{:S(2)}) %all-to-all-start.2) | async-done | bytes 1441824 | tf_op jit(solution)/shard_map/all_to_all | solution.py:69
  78.8 3.7 %all-to-all-start.1 = ((bf16[8,128,1408]{1,0,2:T(8,128)(2,1)}), bf16[8,128,1408]{1,0,2:T(8,128)(2,1)S(1)}, u32[]{:S(2)}, u32[]{:S(2)}) async-start(bf16[8,128,1408]{1,0,2:T(8,128)(2,1)} %pad_maximum_fusion), calls=%async_computation.1 | async-start | bytes 5767168 | tf_op jit(solution)/shard_map/all_to_all | solution.py:30
  82.6 14.6 %all-gather = bf16[16,4,2048]{2,1,0:T(4,128)(2,1)S(1)} all-gather(bf16[1,4,2048]{2,1,0:T(4,128)(2,1)S(1)} %bitcast.28), channel_id=1, replica_groups=mesh['bank'=16,'zero'=16] {'bank'}, dimensions={0}, use_global_device_ids=true | all-gather | bytes 278528 | tf_op jit(solution)/shard_map/all_gather | solution.py:81
  97.2 0.8 reshape.77
  98.0 0.6 constant_dynamic-slice_fusion.2
  98.6 0.7 constant_dynamic-slice_fusion
  99.3 3.0 %copy.52 = bf16[4,88,16,128]{3,2,1,0:T(8,128)(2,1)} copy(bf16[4,88,16,128]{3,0,1,2:T(4,128)(2,1)} %bitcast.4) | data formatting | bytes 2883584 | tf_op jit(solution)/shard_map/all_to_all | solution.py:69
  102.3 3.5 %all_to_all.38 = bf16[4,88,2048]{2,1,0:T(8,128)(2,1)} reshape(bf16[4,88,16,128]{3,2,1,0:T(8,128)(2,1)} %copy.52) | data formatting | bytes 2883584 | tf_op jit(solution)/shard_map/all_to_all | solution.py:69
  105.8 16.3 %all-to-all-done.1 = bf16[8,128,1408]{1,0,2:T(8,128)(2,1)S(1)} async-done(((bf16[8,128,1408]{1,0,2:T(8,128)(2,1)}), bf16[8,128,1408]{1,0,2:T(8,128)(2,1)S(1)}, u32[]{:S(2)}, u32[]{:S(2)}) %all-to-all-start.1) | async-done | bytes 2883616 | tf_op jit(solution)/shard_map/all_to_all | solution.py:30
  122.0 0.4 copy.47
  122.4 0.2 slice_bitcast_fusion
  122.6 1.5 %copy.64 = bf16[4,16,11,8,128]{4,3,1,2,0:T(8,128)(2,1)} copy(bf16[4,16,11,8,128]{4,3,2,1,0:T(8,128)(2,1)S(1)} %get-tuple-element.7) | data formatting | bytes 2883584 | tf_op jit(solution)/shard_map/slice | solution.py:35
  124.1 1.5 %copy.65 = bf16[4,16,11,8,128]{4,3,1,2,0:T(8,128)(2,1)} copy(bf16[4,16,11,8,128]{4,3,2,1,0:T(8,128)(2,1)S(1)} %get-tuple-element.8) | data formatting | bytes 2883584 | tf_op jit(solution)/shard_map/slice | solution.py:35
  (21 shorter events, 0.1 us)
Async XLA Ops:
  0.6 2.7 %copy-start.1 = (f32[4,128,1408]{2,1,0:T(8,128)S(1)}, f32[4,128,1408]{2,1,0:T(8,128)}, u32[]{:S(2)}) copy-start(f32[4,128,1408]{2,1,0:T(8,128)} %param.6) | copy-start | bytes 8650756
  3.6 11.5 %copy-start = (f32[4,128,1408]{2,1,0:T(8,128)S(1)}, f32[4,128,1408]{2,1,0:T(8,128)}, u32[]{:S(2)}) copy-start(f32[4,128,1408]{2,1,0:T(8,128)} %param.5) | copy-start | bytes 8650756
  8.0 25.2 %all-to-all-start = ((f32[16,1,16896]{2,1,0:T(1,128)}), f32[16,1,16896]{2,1,0:T(1,128)}, u32[]{:S(2)}, u32[]{:S(2)}) async-start(f32[16,1,16896]{2,1,0:T(1,128)} %broadcast_in_dim.4), calls=%async_computation | async-start | bytes 2162688 | tf_op jit(solution)/shard_map/all_to_all | solution.py:11
  17.9 4.7 %copy-start.4 = (f32[128,4]{0,1:T(4,128)S(1)}, f32[128,4]{0,1:T(4,128)}, u32[]{:S(2)}) copy-start(f32[128,4]{0,1:T(4,128)} %param.8) | copy-start | bytes 6148
  17.9 4.7 %copy-start.5 = (f32[128]{0:T(128)S(1)}, f32[128]{0:T(128)}, u32[]{:S(2)}) copy-start(f32[128]{0:T(128)} %param.9) | copy-start | bytes 1540
  17.9 22.5 %copy-start.2 = (f32[4,1408,128]{2,1,0:T(8,128)S(1)}, f32[4,1408,128]{2,1,0:T(8,128)}, u32[]{:S(2)}) copy-start(f32[4,1408,128]{2,1,0:T(8,128)} %param.7) | copy-start | bytes 8650756
  33.8 16.7 %all-to-all-start.3 = ((bf16[16,128,4]{1,2,0:T(4,128)(2,1)}), bf16[16,128,4]{1,2,0:T(4,128)(2,1)S(1)}, u32[]{:S(2)}, u32[]{:S(2)}) async-start(bf16[16,128,4]{1,2,0:T(4,128)(2,1)} %broadcast_in_dim.5), calls=%async_computation.3 | async-start | bytes 32768 | tf_op jit(solution)/shard_map/all_to_all | solution.py:11
  48.1 9.6 %copy-start.3 = (f32[4,128,1408]{1,0,2:T(4,128)S(1)}, f32[4,128,1408]{1,0,2:T(4,128)}, u32[]{:S(2)}) copy-start(f32[4,128,1408]{1,0,2:T(4,128)} %copy.44) | copy-start | bytes 8650756
  50.5 28.4 %all-to-all-start.2 = ((bf16[4,1408,128]{2,0,1:T(4,128)(2,1)}), bf16[4,1408,128]{2,0,1:T(4,128)(2,1)}, u32[]{:S(2)}, u32[]{:S(2)}) async-start(bf16[4,1408,128]{2,0,1:T(4,128)(2,1)} %fusion), calls=%async_computation.2 | async-start | bytes 2883584 | tf_op jit(solution)/shard_map/all_to_all | solution.py:69
  78.8 43.2 %all-to-all-start.1 = ((bf16[8,128,1408]{1,0,2:T(8,128)(2,1)}), bf16[8,128,1408]{1,0,2:T(8,128)(2,1)S(1)}, u32[]{:S(2)}, u32[]{:S(2)}) async-start(bf16[8,128,1408]{1,0,2:T(8,128)(2,1)} %pad_maximum_fusion), calls=%async_computation.1 | async-start | bytes 5767168 | tf_op jit(solution)/shard_map/all_to_all | solution.py:30
where the time goes:
time: 126 us
  waiting for transfers between devices  38.8 us (31%)
  local copies, waits for them, and re-layouts  25.8 us (20%)
  other arithmetic  24.1 us (19%)
  starting transfers between devices  21.5 us (17%)
  blocking collectives  14.6 us (12%)
    all_to_all x1, waiting for transfers between devices, side_by_side(): lax.all_to_all(both, axis, split_axis=split_dim, concat_axis=concat_dim,...  16.3 us
    all_gather x1, blocking collectives, local(): serve_router = lax.all_gather(row_router, 'bank', axis=1, tiled=True)  14.6 us
    all_to_all x1, waiting for transfers between devices, local(): lax.all_to_all(narrow_down, 'zero', split_axis=1, concat_axis=2, tiled=True)  12 us
    all_to_all x2, waiting for transfers between devices, copy_for_each(): lax.all_to_all(jnp.broadcast_to(x[None], (count, *x.shape)), axis, 0, 0,...  10.6 us
    all_to_all x2, starting transfers between devices, copy_for_each(): lax.all_to_all(jnp.broadcast_to(x[None], (count, *x.shape)), axis, 0, 0,...  10.6 us
    unnamed x16, local copies, waits for them, and re-layouts  8.94 us
    convert_element_type x1, other arithmetic, local(): (master_down / jnp.expand_dims(scale_down, 2)).astype(jnp.bfloat16)  7.73 us
    all_to_all x1, starting transfers between devices, local(): lax.all_to_all(narrow_down, 'zero', split_axis=1, concat_axis=2, tiled=True)  7.2 us
  transfers between devices with their start and end apart: 4, of which 3 were waited for; matrix products, arithmetic and copies ran while one was open for 28% of the time, Pallas kernels for 0%

commit v1 on v0

v1 whole, which is shorter than its diff:
```python
import jax
import jax.numpy as jnp
from jax import lax
from jax.experimental import pallas as pl
from jax.experimental.pallas import tpu as pltpu
from jax.sharding import PartitionSpec as P

D_MODEL = 2048
LANES = 128
TINY = 1e-25
REACH = 2.0**0.9


def coded(v):
    for _ in range(4):
        v = v * jnp.abs(v)
    return v


def decoded(y):
    a = jnp.abs(y)
    r = jnp.exp(jnp.log(jnp.maximum(a, 1e-38)) * (1 / 16))
    return jnp.where(y > 0, r, jnp.where(y < 0, -r, 0.0))


def in_two(p):
    high = p.astype(jnp.bfloat16).astype(jnp.float32)
    low = (p - high).astype(jnp.bfloat16).astype(jnp.float32)
    return high, low


def normaliser(p):
    return (LANES * REACH) / jnp.maximum(p, TINY)


def encode_body(gate, up, down, out, sums, cols, *, groups, rows, experts):
    k = pl.program_id(0)
    across = lax.broadcasted_iota(jnp.int32, (rows, LANES), 1)

    def turned(x):
        p = jnp.sum(jnp.abs(x), axis=0, keepdims=True)
        high, low = in_two(p)
        y = coded(x * normaliser(high + low))
        yt = y.T
        for d in range(groups):
            out[d] = yt[d * rows : (d + 1) * rows].astype(jnp.bfloat16)
        sums[pl.ds(2 * k, 1)] = high
        sums[pl.ds(2 * k + 1, 1)] = low

    @pl.when(k < experts)
    def _():
        turned(gate[0])

    @pl.when((k >= experts) & (k < 2 * experts))
    def _():
        turned(up[0])

    @pl.when((k >= 2 * experts) & (k < 3 * experts))
    def _():
        e = k - 2 * experts
        for d in range(groups):
            x = down[0, d * rows : (d + 1) * rows]
            p = jnp.sum(jnp.abs(x), axis=1, keepdims=True)
            high, low = in_two(p)
            out[d] = coded(x * normaliser(high + low)).astype(jnp.bfloat16)
            both = jnp.where(across == 2 * e, high, jnp.where(across == 2 * e + 1, low, 0.0))
            cols[d] = jnp.where(e == 0, both, cols[d] + both)

    @pl.when(k == 3 * experts)
    def _():
        for d in range(groups):
            turned_sums = sums[:, d * rows : (d + 1) * rows]
            down_sums = cols[d].T[: 2 * experts]
            both = jnp.concatenate([turned_sums, down_sums], axis=0)
            both = jnp.pad(both, ((0, 0), (0, LANES - rows)))
            out[d, : 6 * experts] = both.astype(jnp.bfloat16)


def encode(gate, up, down, groups):
    experts, part, inner = gate.shape
    rows = inner // groups
    total = 3 * experts * rows + 6 * experts

    def block(first):
        return lambda k: (jnp.clip(k - first, 0, experts - 1), 0, 0)

    def body(*refs):
        encode_body(*refs, groups=groups, rows=rows, experts=experts)

    return pl.pallas_call(
        body,
        grid=(3 * experts + 1,),
        in_specs=[
            pl.BlockSpec((1, part, inner), block(0)),
            pl.BlockSpec((1, part, inner), block(experts)),
            pl.BlockSpec((1, inner, part), block(2 * experts)),
        ],
        out_specs=pl.BlockSpec((groups, rows, LANES), lambda k: (0, k, 0)),
        out_shape=jax.ShapeDtypeStruct((groups, total, LANES), jnp.bfloat16),
        scratch_shapes=[
            pltpu.VMEM((4 * experts, inner), jnp.float32),
            pltpu.VMEM((groups, rows, LANES), jnp.float32),
        ],
        name="encode",
    )(gate, up, down)


def decode_body(data, sums, gate, up, down, scales, factor, *, groups, rows, experts):
    k = pl.program_id(0)
    n = 3 * experts

    @pl.when(k == 0)
    def _():
        own = []
        for s in range(groups):
            words = sums[s].astype(jnp.float32)
            own.append(words.reshape(n, 2, LANES).sum(axis=1))
        scale = sum(own) / D_MODEL
        scales[...] = scale
        scale = jnp.where(scale > 0, scale, 1.0)
        for s in range(groups):
            f = jnp.maximum(own[s], TINY) / (LANES * REACH) / scale
            f = jnp.pad(f, ((0, LANES - n), (0, 0)))
            factor[s] = f.T

    column = lax.broadcasted_iota(jnp.int32, (LANES, LANES), 1)
    for s in range(groups):
        f = jnp.sum(jnp.where(column == k, factor[s], 0.0), axis=1, keepdims=True)[:rows]
        y = (decoded(data[s].astype(jnp.float32)) * f).astype(jnp.bfloat16)
        at = slice(s * LANES, (s + 1) * LANES)

        @pl.when(k < experts)
        def _():
            gate[0, :, at] = y

        @pl.when((k >= experts) & (k < 2 * experts))
        def _():
            up[0, :, at] = y

        @pl.when(k >= 2 * experts)
        def _():
            down[0, :, at] = y


def decode(received, experts, rows):
    groups = received.shape[0]
    n = 3 * experts

    def block(first):
        return lambda k: (jnp.clip(k - first, 0, experts - 1), 0, 0)

    def body(*refs):
        decode_body(*refs, groups=groups, rows=rows, experts=experts)

    final = jax.ShapeDtypeStruct((experts, rows, groups * LANES), jnp.bfloat16)
    return pl.pallas_call(
        body,
        grid=(n,),
        in_specs=[
            pl.BlockSpec((groups, rows, LANES), lambda k: (0, k, 0)),
            pl.BlockSpec((groups, 2 * n, LANES), lambda k: (0, n * rows // (2 * n), 0)),
        ],
        out_specs=[
            pl.BlockSpec((1, rows, groups * LANES), block(0)),
            pl.BlockSpec((1, rows, groups * LANES), block(experts)),
            pl.BlockSpec((1, rows, groups * LANES), block(2 * experts)),
            pl.BlockSpec((n, LANES), lambda k: (0, 0)),
        ],
        out_shape=[final, final, final, jax.ShapeDtypeStruct((n, LANES), jnp.float32)],
        scratch_shapes=[pltpu.VMEM((groups, LANES, LANES), jnp.float32)],
        name="decode",
    )(received, received)


def local(master_gate, master_up, master_down, router_weight, router_gain):
    groups = lax.axis_size("zero")
    experts, _, inner = master_gate.shape
    rows = inner // groups
    sent = encode(master_gate, master_up, master_down, groups)
    received = lax.all_to_all(sent, "zero", 0, 0, tiled=True)
    gate, up, down, scales = decode(received, experts, rows)
    part = (router_weight * router_gain[:, None]).astype(jnp.bfloat16).T
    row = lax.all_gather(part, "zero", axis=1, tiled=True)
    router = lax.all_gather(row, "bank", axis=0, tiled=True)
    scale = scales[:, :rows]
    return (
        jnp.swapaxes(gate, 1, 2),
        jnp.swapaxes(up, 1, 2),
        down,
        scale[:experts],
        scale[experts : 2 * experts],
        scale[2 * experts :],
        router.T,
    )


def solution(mesh):
    placed = (
        P("bank", "zero", None),
        P("bank", "zero", None),
        P("bank", None, "zero"),
        P("zero", "bank"),
        P("zero"),
    )
    return jax.shard_map(
        local,
        mesh=mesh,
        in_specs=placed,
        out_specs=(
            P("bank", None, "zero"),
            P("bank", None, "zero"),
            P("bank", "zero", None),
            P("bank", "zero"),
            P("bank", "zero"),
            P("bank", "zero"),
            P(),
        ),
        check_vma=False,
    )
```

time: 126 us -> 146 us (1.16)
  the two profiles are of different devices: /device:TPU:224 before, /device:TPU:1 now
where the time goes in v1:
time: 146 us; the launch traced here: 145 us
  blocking collectives  101 us (69%)
  Pallas kernels  34 us (23%)
  starting transfers between devices  7.75 us (5%)
  local copies, waits for them, and re-layouts  2.11 us (1%)
    all_gather x1, blocking collectives, local(): row = lax.all_gather(part, 'zero', axis=1, tiled=True)  75 us
    all_gather x1, blocking collectives, local(): router = lax.all_gather(row, 'bank', axis=0, tiled=True)  25.8 us
    pallas_call x1, Pallas kernels, decode(): pl.pallas_call(body, grid=(n,), in_specs=[pl.BlockSpec((groups, rows, LAN...  21 us
    pallas_call x1, Pallas kernels, encode(): pl.pallas_call(body, grid=(3 * experts + 1,), in_specs=[pl.BlockSpec((1,...  13 us
    all_to_all x1, starting transfers between devices, local(): received = lax.all_to_all(sent, 'zero', 0, 0, tiled=True)  7.75 us
  transfers between devices with their start and end apart: 1, of which 0 were waited for; matrix products, arithmetic and copies ran while one was open for 1% of the time, Pallas kernels for 0%

profile of v1, /device:TPU:1, one launch (start us, length us, event | category | flops | bytes accessed | tf_op | source)
XLA Modules:
  0.0 145.3 jit_solution(6397117316522863562)
XLA Ops:
  0.6 13.0 %encode.1 = bf16[16,1080,128]{2,1,0:T(8,128)(2,1)} custom-call(f32[4,128,1408]{2,1,0:T(8,128)} %refs_0_.1, f32[4,128,1408]{2,1,0:T(8,128)} %refs_1_.1, f32[4,1408,128]{2,1,0:T(8,128)} %refs_2_.1), custom_call_target="tpu_custom_call" | custom-call | tf_op jit(solution)/shard_map/encode/pallas_call | solution.py:90
  13.6 0.0 copy-start
  13.6 0.0 copy-start.1
  13.6 7.7 %all-to-all-start = ((bf16[16,1080,128]{2,1,0:T(8,128)(2,1)}), bf16[16,1080,128]{2,1,0:T(8,128)(2,1)}, u32[]{:S(2)}, u32[]{:S(2)}) async-start(bf16[16,1080,128]{2,1,0:T(8,128)(2,1)} %encode.1), calls=%async_computation | async-start | bytes 8847360 | tf_op jit(solution)/shard_map/all_to_all | solution.py:180
  21.4 0.0 copy-done
  21.4 0.0 copy-done.1
  21.4 75.0 %all_gather.6 = bf16[4,2048]{1,0:T(4,128)(2,1)S(1)} all-gather(bf16[4,128]{1,0:T(4,128)(2,1)S(1)} %fusion), channel_id=1, replica_groups=mesh['bank'=16,'zero'=16] {'zero'}, dimensions={1}, use_global_device_ids=true | all-gather | bytes 17408 | tf_op jit(solution)/shard_map/all_gather | solution.py:183
  96.4 25.8 %all-gather = bf16[16,4,2048]{2,1,0:T(4,128)(2,1)S(1)} all-gather(bf16[1,4,2048]{2,1,0:T(4,128)(2,1)S(1)} %bitcast.7), channel_id=1, replica_groups=mesh['bank'=16,'zero'=16] {'bank'}, dimensions={0}, use_global_device_ids=true | all-gather | bytes 278528 | tf_op jit(solution)/shard_map/all_gather | solution.py:184
  122.2 0.8 reshape.16
  123.0 0.0 all-to-all-done.refs_0_.refs_1_
  123.0 21.0 %decode.1 = (bf16[4,88,2048]{2,1,0:T(8,128)(2,1)}, bf16[4,88,2048]{2,1,0:T(8,128)(2,1)}, bf16[4,88,2048]{2,1,0:T(8,128)(2,1)}, f32[12,128]{1,0:T(8,128)}) custom-call(bf16[16,1080,128]{2,1,0:T(8,128)(2,1)} %all-to-all-done.refs_0_.refs_1_, bf16[16,1080,128]{2,1,0:T(8,128)(2,1)} %all-to-all-done.refs_0_.refs_1_), custom_call_target="tpu_custom_call" | custom-call | tf_op jit(solution)/shard_map/decode/pallas_call | solution.py:156
  144.0 1.3 fusion.1
  (1 shorter events, 0.0 us)
Async XLA Ops:
  13.6 7.8 %copy-start = (f32[128,4]{0,1:T(4,128)S(1)}, f32[128,4]{0,1:T(4,128)}, u32[]{:S(2)}) copy-start(f32[128,4]{0,1:T(4,128)} %param.8) | copy-start | bytes 6148
  13.6 7.8 %copy-start.1 = (f32[128]{0:T(128)S(1)}, f32[128]{0:T(128)}, u32[]{:S(2)}) copy-start(f32[128]{0:T(128)} %param.9) | copy-start | bytes 1540
  13.6 109.3 %all-to-all-start = ((bf16[16,1080,128]{2,1,0:T(8,128)(2,1)}), bf16[16,1080,128]{2,1,0:T(8,128)(2,1)}, u32[]{:S(2)}, u32[]{:S(2)}) async-start(bf16[16,1080,128]{2,1,0:T(8,128)(2,1)} %encode.1), calls=%async_computation | async-start | bytes 8847360 | tf_op jit(solution)/shard_map/all_to_all | solution.py:180

commit v2 on v0

v2 whole, which is shorter than its diff:
```python
import jax
import jax.numpy as jnp
from jax import lax
from jax.experimental import pallas as pl
from jax.experimental.pallas import tpu as pltpu
from jax.sharding import PartitionSpec as P

D_MODEL = 2048
LANES = 128
POWER = 15
TINY = 1e-25
REACH = LANES * 2.0**1.5
ACROSS = (((1,), (1,)), ((), ()))
SIDE = 4
SHIFTS = (
    (0, 1), (0, 3), (1, 0), (3, 0), (1, 1), (3, 3), (1, 3), (3, 1),
    (0, 2), (2, 0), (1, 2), (2, 1), (3, 2), (2, 3), (2, 2),
)


def partner(i, shift, sign):
    y = (i // SIDE + sign * shift[0]) % SIDE
    return y * SIDE + (i % SIDE + sign * shift[1]) % SIDE


def partners(me, sign):
    low = SIDE - 1
    found = [me]
    for dy, dx in SHIFTS:
        y = (me + SIDE * ((sign * dy) & low)) & (SIDE * low)
        found.append(y | ((me + ((sign * dx) & low)) & low))
    return found


def coded(v):
    cube = v * v * v
    sixth = cube * cube
    return (sixth * sixth * cube).astype(jnp.bfloat16)


def restored(y, factor):
    size = jnp.maximum(jnp.abs(y), 1e-37)
    return y * jnp.exp2(jnp.log2(size) * (1 / POWER - 1)) * factor


def in_two(p):
    high = p.astype(jnp.bfloat16).astype(jnp.float32)
    low = (p - high).astype(jnp.bfloat16).astype(jnp.float32)
    return high, low


def own_sums(x, axis):
    high, low = in_two(jnp.sum(jnp.abs(x), axis=axis, keepdims=True))
    return high, low, REACH / jnp.maximum(high + low, TINY)


def identity(rows):
    shape = (rows, LANES)
    eye = lax.broadcasted_iota(jnp.int32, shape, 0) == lax.broadcasted_iota(jnp.int32, shape, 1)
    return eye.astype(jnp.float32).astype(jnp.bfloat16)


def encode_body(me, *refs, groups, rows, experts):
    given, outs = refs[:3], refs[3 : 3 + groups]
    held = refs[3 + groups : 6 + groups]
    stage, turned, sums, cols, arrived, left = refs[6 + groups :]
    inner = groups * rows
    part = experts * rows
    dest = [pl.multiple_of(d * rows, 8) for d in partners(me[0], 1)]

    def fetch(a, e):
        return pltpu.make_async_copy(given[a].at[e], held[a].at[e], arrived.at[a, e])

    def send(t, first, last):
        at = pl.ds(first, last - first)
        pltpu.make_async_copy(stage.at[t, at], outs[t].at[at], left.at[t]).start()

    for a in range(3):
        for e in range(experts):
            fetch(a, e).start()

    def turn(a):
        def one(e, _):
            fetch(a, e).wait()
            x = held[a][e]
            high, low, norm = own_sums(x, 0)
            y = coded(x * norm)
            eye = identity(LANES)
            for b in range(inner // LANES):
                at = slice(b * LANES, (b + 1) * LANES)
                turned[at] = lax.dot_general(eye, y[:, at], ACROSS, preferred_element_type=jnp.float32)
            k = a * experts + e
            for t in range(groups):
                at = pl.ds(pl.multiple_of(k * rows, 8), rows)
                stage[t, at] = turned[pl.ds(dest[t], rows)].astype(jnp.bfloat16)
            sums[pl.ds(k, 1)] = high
            sums[pl.ds(2 * experts + k, 1)] = low
            return 0

        lax.fori_loop(0, experts, one, 0)
        for t in range(groups):
            send(t, a * part, (a + 1) * part)

    turn(0)
    turn(1)
    lane = lax.broadcasted_iota(jnp.int32, (rows, LANES), 1)

    def keep(e, _):
        fetch(2, e).wait()
        for t in range(groups):
            x = held[2][e, pl.ds(dest[t], rows)]
            high, low, norm = own_sums(x, 1)
            at = pl.ds(pl.multiple_of((2 * experts + e) * rows, 8), rows)
            stage[t, at] = coded(x * norm)
            cols[t] = jnp.where(lane == e, high, jnp.where(lane == experts + e, low, cols[t]))
        return 0

    lax.fori_loop(0, experts, keep, 0)
    n = 2 * experts
    for d in range(groups):
        some = sums[:, d * rows : (d + 1) * rows]
        turned[d * rows : d * rows + 2 * n] = jnp.pad(some, ((0, 0), (0, LANES - rows)))
    for t in range(groups):
        own = jnp.where(lane < n, cols[t], 0.0).astype(jnp.bfloat16)
        own = lax.dot_general(identity(n), own, ACROSS, preferred_element_type=jnp.float32)
        own = jnp.pad(own, ((0, 0), (0, LANES - rows)))
        both = jnp.concatenate([turned[pl.ds(dest[t], 2 * n)], own], axis=0)
        stage[t, 3 * part :] = both.astype(jnp.bfloat16)
        send(t, 2 * part, 3 * part + 3 * n)
    for t in range(groups):
        pltpu.make_async_copy(stage.at[t], outs[t], left.at[t]).wait()


def encode(gate, up, down, me, groups):
    experts, _, inner = gate.shape
    rows = inner // groups
    total = 3 * experts * rows + 6 * experts

    def body(*refs):
        encode_body(*refs, groups=groups, rows=rows, experts=experts)

    anywhere = pl.BlockSpec(memory_space=pl.ANY)
    return pl.pallas_call(
        body,
        in_specs=[pl.BlockSpec(memory_space=pltpu.SMEM)] + [anywhere] * 3,
        out_specs=[anywhere] * groups,
        out_shape=[jax.ShapeDtypeStruct((total, LANES), jnp.bfloat16)] * groups,
        scratch_shapes=[
            pltpu.VMEM(gate.shape, jnp.float32),
            pltpu.VMEM(up.shape, jnp.float32),
            pltpu.VMEM(down.shape, jnp.float32),
            pltpu.VMEM((groups, total, LANES), jnp.bfloat16),
            pltpu.VMEM((inner, LANES), jnp.float32),
            pltpu.VMEM((4 * experts, inner), jnp.float32),
            pltpu.VMEM((groups, rows, LANES), jnp.float32),
            pltpu.SemaphoreType.DMA((3, experts)),
            pltpu.SemaphoreType.DMA((groups,)),
        ],
        name="encode",
    )(me, gate, up, down)


def decode_body(me, *refs, groups, rows, experts):
    data, outs = refs[:groups], refs[groups : groups + 3]
    scales, stage, factor, left = refs[groups + 3 :]
    source = [pl.multiple_of(d * LANES, LANES) for d in partners(me[0], -1)]
    n = 3 * experts
    m = 2 * experts
    own = []
    for g in range(groups):
        words = data[g][n * rows :].astype(jnp.float32)
        turned = words[:m] + words[m : 2 * m]
        kept = words[2 * m : 2 * m + experts] + words[2 * m + experts :]
        own.append((turned, kept))
    for first, size, parts in ((0, m, [o[0] for o in own]), (m, experts, [o[1] for o in own])):
        scale = sum(parts) / D_MODEL
        scales[first : first + size] = scale
        scale = 1 / (REACH * jnp.where(scale > 0, scale, 1.0))
        for g in range(groups):
            factor[first : first + size, g] = jnp.maximum(parts[g], TINY) * scale

    def copy(a, e):
        return pltpu.make_async_copy(stage.at[a, e], outs[a].at[e], left.at[a, e])

    for a in range(3):

        def one(e, _, a=a):
            k = a * experts + e
            f = factor[k].T
            for g in range(groups):
                y = data[g][pl.ds(pl.multiple_of(k * rows, 8), rows)].astype(jnp.float32)
                y = restored(y, f[:rows, g : g + 1])
                stage[a, e, :, pl.ds(source[g], LANES)] = y.astype(jnp.bfloat16)
            copy(a, e).start()
            return 0

        lax.fori_loop(0, experts, one, 0)
    for a in range(3):
        for e in range(experts):
            copy(a, e).wait()


def decode(pieces, me, experts, rows):
    groups = len(pieces)
    n = 3 * experts

    def body(*refs):
        decode_body(*refs, groups=groups, rows=rows, experts=experts)

    final = jax.ShapeDtypeStruct((experts, rows, groups * LANES), jnp.bfloat16)
    anywhere = pl.BlockSpec(memory_space=pl.ANY)
    here = pl.BlockSpec(memory_space=pltpu.VMEM)
    return pl.pallas_call(
        body,
        in_specs=[pl.BlockSpec(memory_space=pltpu.SMEM)] + [here] * groups,
        out_specs=[anywhere, anywhere, anywhere, here],
        out_shape=[final, final, final, jax.ShapeDtypeStruct((n, LANES), jnp.float32)],
        scratch_shapes=[
            pltpu.VMEM((3, experts, rows, groups * LANES), jnp.bfloat16),
            pltpu.VMEM((n, groups, LANES), jnp.float32),
            pltpu.SemaphoreType.DMA((3, experts)),
        ],
        compiler_params=pltpu.CompilerParams(vmem_limit_bytes=10 << 20),
        name="decode",
    )(me, *pieces)


def rolled(parts, by):
    rows = sum(p.shape[0] for p in parts)

    def body(by, *refs):
        x = jnp.concatenate([r[...].astype(jnp.float32) for r in refs[:-1]], axis=0)
        refs[-1][...] = pltpu.roll(x, by[0], 0).astype(jnp.bfloat16)

    return pl.pallas_call(
        body,
        in_specs=[pl.BlockSpec(memory_space=pltpu.SMEM)]
        + [pl.BlockSpec(memory_space=pltpu.VMEM)] * len(parts),
        out_specs=pl.BlockSpec(memory_space=pltpu.VMEM),
        out_shape=jax.ShapeDtypeStruct((rows, parts[0].shape[1]), jnp.bfloat16),
        compiler_params=pltpu.CompilerParams(vmem_limit_bytes=4 << 20),
        name="rolled",
    )(by, *parts)


def gathered(x, axis):
    count, n = lax.axis_size(axis), 1
    rows, parts = x.shape[0], [x]
    while n < count:
        perm = [((i + n) % count, i) for i in range(count)]
        parts.append(lax.ppermute(jnp.concatenate(parts, axis=0), axis, perm))
        n *= 2
    return rolled(parts, (lax.axis_index(axis) * rows).astype(jnp.int32).reshape(1))


def local(master_gate, master_up, master_down, router_weight, router_gain):
    groups = lax.axis_size("zero")
    experts, _, inner = master_gate.shape
    rows = inner // groups
    me = lax.axis_index("zero").astype(jnp.int32).reshape(1)
    sent = encode(master_gate, master_up, master_down, me, groups)
    pieces = [sent[0]]
    for t, s in enumerate(SHIFTS):
        perm = [(i, partner(i, s, 1)) for i in range(groups)]
        pieces.append(lax.ppermute(sent[t + 1], "zero", perm))
    gate, up, down, scales = decode(pieces, me, experts, rows)
    part = (router_weight * router_gain[:, None]).astype(jnp.bfloat16).T
    copies = jnp.broadcast_to(part[None], (groups, *part.shape))
    row = lax.all_to_all(copies, "zero", 0, 0, tiled=True)
    row = jnp.swapaxes(row, 0, 1).reshape(part.shape[0], -1)
    router = gathered(row, "bank")
    scale = scales[:, :rows]
    return (
        jnp.swapaxes(gate, 1, 2),
        jnp.swapaxes(up, 1, 2),
        down,
        scale[:experts],
        scale[experts : 2 * experts],
        scale[2 * experts :],
        router.T,
    )


def solution(mesh):
    placed = (
        P("bank", "zero", None),
        P("bank", "zero", None),
        P("bank", None, "zero"),
        P("zero", "bank"),
        P("zero"),
    )
    return jax.shard_map(
        local,
        mesh=mesh,
        in_specs=placed,
        out_specs=(
            P("bank", None, "zero"),
            P("bank", None, "zero"),
            P("bank", "zero", None),
            P("bank", "zero"),
            P("bank", "zero"),
            P("bank", "zero"),
            P(),
        ),
        check_vma=False,
    )
```

time: 126 us -> 121 us (0.960)
  other arithmetic: 24.1 us -> 0.77 us
  local copies, waits for them, and re-layouts: 25.8 us -> 3.11 us
  Pallas kernels: 0 us -> 16.2 us
  waiting for transfers between devices: 38.8 us -> 53.1 us
  starting transfers between devices: 21.5 us -> 32.6 us
    ppermute x0 -> x19, waiting for transfers between devices: none -> 53.1 us  [the longest x15 41.2 us: local(): pieces.append(lax.ppermute(sent[t + 1], 'zero', perm))]
    all_to_all x4 -> x0, waiting for transfers between devices: 38.8 us -> none  [the longest x1 16.3 us: side_by_side(): lax.all_to_all(both, axis, split_axis=split_dim, concat_axis=concat_dim,...]
    ppermute x0 -> x19, starting transfers between devices: none -> 32.6 us  [the longest x15 29.9 us: local(): pieces.append(lax.ppermute(sent[t + 1], 'zero', perm))]
    all_to_all x4 -> x0, starting transfers between devices: 21.5 us -> none  [the longest x2 10.6 us: copy_for_each(): lax.all_to_all(jnp.broadcast_to(x[None], (count, *x.shape)), axis, 0, 0,...]
    pallas_call x0 -> x3, Pallas kernels: none -> 16.2 us  [the longest x1 8.55 us: encode(): pl.pallas_call(body, in_specs=[pl.BlockSpec(memory_space=pltpu.SMEM)] + [...]
    all_gather x1 -> x0, blocking collectives: 14.6 us -> none  [local(): serve_router = lax.all_gather(row_router, 'bank', axis=1, tiled=True)]
    all_to_all x0 -> x1, blocking collectives: none -> 14.4 us  [local(): row = lax.all_to_all(copies, 'zero', 0, 0, tiled=True)]
    convert_element_type x3 -> x0, other arithmetic: 14.3 us -> none  [the longest x1 7.73 us: local(): (master_down / jnp.expand_dims(scale_down, 2)).astype(jnp.bfloat16)]
  transfers between devices with their start and end apart: 4 -> 19, of which waited for: 3 -> 11; matrix products, arithmetic and copies ran while one was open for 28% -> 0% of each run, Pallas kernels for 0% -> 8%
where the time goes in v2:
time: 121 us
  waiting for transfers between devices  53.1 us (44%)
  starting transfers between devices  32.6 us (27%)
  Pallas kernels  16.2 us (13%)
  blocking collectives  14.4 us (12%)
  local copies, waits for them, and re-layouts  3.11 us (3%)
    ppermute x15, waiting for transfers between devices, local(): pieces.append(lax.ppermute(sent[t + 1], 'zero', perm))  41.2 us
    ppermute x15, starting transfers between devices, local(): pieces.append(lax.ppermute(sent[t + 1], 'zero', perm))  29.9 us
    all_to_all x1, blocking collectives, local(): row = lax.all_to_all(copies, 'zero', 0, 0, tiled=True)  14.4 us
    ppermute x4, waiting for transfers between devices, gathered(): parts.append(lax.ppermute(jnp.concatenate(parts, axis=0), axis, perm))  12 us
    pallas_call x1, Pallas kernels, encode(): pl.pallas_call(body, in_specs=[pl.BlockSpec(memory_space=pltpu.SMEM)] + [...  8.55 us
    pallas_call x1, Pallas kernels, decode(): pl.pallas_call(body, in_specs=[pl.BlockSpec(memory_space=pltpu.SMEM)] + [...  6.85 us
    ppermute x4, starting transfers between devices, gathered(): parts.append(lax.ppermute(jnp.concatenate(parts, axis=0), axis, perm))  2.72 us
    unnamed x6, local copies, waits for them, and re-layouts  2.51 us
  transfers between devices with their start and end apart: 19, of which 11 were waited for; matrix products, arithmetic and copies ran while one was open for 0% of the time, Pallas kernels for 8%

profile of v2, /device:TPU:224, one launch (start us, length us, event | category | flops | bytes accessed | tf_op | source)
XLA Modules:
  0.0 121.0 jit_solution(835750174086044964)
XLA Ops:
  0.6 0.7 fusion
  1.3 14.4 %all_to_all.5 = bf16[16,4,128]{2,1,0:T(4,128)(2,1)S(1)} all-to-all(bf16[16,4,128]{2,1,0:T(4,128)(2,1)S(1)} %broadcast_in_dim.2), channel_id=1, replica_groups=mesh['bank'=16,'zero'=16] {'zero'}, dimensions={0} | all-to-all | bytes 32768 | tf_op jit(solution)/shard_map/all_to_all | solution.py:269
  15.8 1.4 %collective-permute-done.15.refs_1_ = bf16[4,2048]{1,0:T(4,128)(2,1)S(1)} collective-permute-done((bf16[4,2048]{1,0:T(4,128)(2,1)S(1)}, bf16[4,2048]{1,0:T(4,128)(2,1)S(1)}, u32[]{:S(2)}, u32[]{:S(2)}) %collective-permute-start.15) | collective-permute-done | bytes 16416 | tf_op jit(solution)/shard_map/ppermute | solution.py:251
  17.2 1.1 collective-permute-start.16
  18.3 4.1 %collective-permute-done.16.refs_2_ = bf16[8,2048]{1,0:T(8,128)(2,1)S(1)} collective-permute-done((bf16[8,2048]{1,0:T(8,128)(2,1)S(1)}, bf16[8,2048]{1,0:T(8,128)(2,1)S(1)}, u32[]{:S(2)}, u32[]{:S(2)}) %collective-permute-start.16) | collective-permute-done | bytes 32800 | tf_op jit(solution)/shard_map/ppermute | solution.py:251
  22.5 0.5 collective-permute-start.17
  23.0 6.4 %collective-permute-done.17.refs_3_ = bf16[16,2048]{1,0:T(8,128)(2,1)S(1)} collective-permute-done((bf16[16,2048]{1,0:T(8,128)(2,1)S(1)}, bf16[16,2048]{1,0:T(8,128)(2,1)S(1)}, u32[]{:S(2)}, u32[]{:S(2)}) %collective-permute-start.17) | collective-permute-done | bytes 65568 | tf_op jit(solution)/shard_map/ppermute | solution.py:251
  29.4 1.1 collective-permute-start.18
  30.6 8.6 %encode.1 = (bf16[1080,128]{1,0:T(8,128)(2,1)}, bf16[1080,128]{1,0:T(8,128)(2,1)}, bf16[1080,128]{1,0:T(8,128)(2,1)}, bf16[1080,128]{1,0:T(8,128)(2,1)}, bf16[10...) custom-call(s32[1]{0:T(128)} %bitcast.refs_0_, ...), custom_call_target="tpu_custom_call" | custom-call | tf_op jit(solution)/shard_map/encode/pallas_call | solution.py:143
  39.1 0.6 collective-permute-start
  39.8 2.7 %collective-permute-start.1 = (bf16[1080,128]{1,0:T(8,128)(2,1)}, bf16[1080,128]{1,0:T(8,128)(2,1)S(1)}, u32[]{:S(2)}, u32[]{:S(2)}) collective-permute-start(bf16[1080,128]{1,0:T(8,128)(2,1)} %get-tuple-element.29), channel_id=1, source_target_pairs={{0,3},{1,0},{2,1},{3,2},{4,7},{5,4},{6,5},{7,6},{8,11},{9,8},{10,9... | collective-permute-start | bytes 829448 | tf_op jit(solution)/shard_map/ppermute | solution.py:265
  42.4 2.4 %collective-permute-start.11 = (bf16[1080,128]{1,0:T(8,128)(2,1)}, bf16[1080,128]{1,0:T(8,128)(2,1)S(1)}, u32[]{:S(2)}, u32[]{:S(2)}) collective-permute-start(bf16[1080,128]{1,0:T(8,128)(2,1)} %get-tuple-element.39), channel_id=1, source_target_pairs={{0,9},{1,10},{2,11},{3,8},{4,13},{5,14},{6,15},{7,12},{8,1},{9,2},... | collective-permute-start | bytes 829448 | tf_op jit(solution)/shard_map/ppermute | solution.py:265
  44.8 0.7 copy-done.1
  45.4 3.3 %collective-permute-start.12 = (bf16[1080,128]{1,0:T(8,128)(2,1)}, bf16[1080,128]{1,0:T(8,128)(2,1)S(1)}, u32[]{:S(2)}, u32[]{:S(2)}) collective-permute-start(bf16[1080,128]{1,0:T(8,128)(2,1)} %get-tuple-element.40), channel_id=1, source_target_pairs={{0,14},{1,15},{2,12},{3,13},{4,2},{5,3},{6,0},{7,1},{8,6},{9,7},{1... | collective-permute-start | bytes 829448 | tf_op jit(solution)/shard_map/ppermute | solution.py:265
  48.7 6.7 %collective-permute-done.refs_2_ = bf16[1080,128]{1,0:T(8,128)(2,1)S(1)} collective-permute-done((bf16[1080,128]{1,0:T(8,128)(2,1)}, bf16[1080,128]{1,0:T(8,128)(2,1)S(1)}, u32[]{:S(2)}, u32[]{:S(2)}) %collective-permute-start) | collective-permute-done | bytes 276512 | tf_op jit(solution)/shard_map/ppermute | solution.py:265
  55.4 3.2 %collective-permute-done.1.refs_3_ = bf16[1080,128]{1,0:T(8,128)(2,1)S(1)} collective-permute-done((bf16[1080,128]{1,0:T(8,128)(2,1)}, bf16[1080,128]{1,0:T(8,128)(2,1)S(1)}, u32[]{:S(2)}, u32[]{:S(2)}) %collective-permute-start.1) | collective-permute-done | bytes 276512 | tf_op jit(solution)/shard_map/ppermute | solution.py:265
  58.9 3.7 %collective-permute-done.11.refs_13_ = bf16[1080,128]{1,0:T(8,128)(2,1)S(1)} collective-permute-done((bf16[1080,128]{1,0:T(8,128)(2,1)}, bf16[1080,128]{1,0:T(8,128)(2,1)S(1)}, u32[]{:S(2)}, u32[]{:S(2)}) %collective-permute-start.11) | collective-permute-done | bytes 276512 | tf_op jit(solution)/shard_map/ppermute | solution.py:265
  62.6 3.4 %collective-permute-start.3 = (bf16[1080,128]{1,0:T(8,128)(2,1)}, bf16[1080,128]{1,0:T(8,128)(2,1)S(1)}, u32[]{:S(2)}, u32[]{:S(2)}) collective-permute-start(bf16[1080,128]{1,0:T(8,128)(2,1)} %get-tuple-element.31), channel_id=1, source_target_pairs={{0,12},{1,13},{2,14},{3,15},{4,0},{5,1},{6,2},{7,3},{8,4},{9,5},{1... | collective-permute-start | bytes 829448 | tf_op jit(solution)/shard_map/ppermute | solution.py:265
  66.0 8.1 %collective-permute-done.12.refs_14_ = bf16[1080,128]{1,0:T(8,128)(2,1)S(1)} collective-permute-done((bf16[1080,128]{1,0:T(8,128)(2,1)}, bf16[1080,128]{1,0:T(8,128)(2,1)S(1)}, u32[]{:S(2)}, u32[]{:S(2)}) %collective-permute-start.12) | collective-permute-done | bytes 276512 | tf_op jit(solution)/shard_map/ppermute | solution.py:265
  74.1 5.3 %collective-permute-start.5 = (bf16[1080,128]{1,0:T(8,128)(2,1)}, bf16[1080,128]{1,0:T(8,128)(2,1)S(1)}, u32[]{:S(2)}, u32[]{:S(2)}) collective-permute-start(bf16[1080,128]{1,0:T(8,128)(2,1)} %get-tuple-element.33), channel_id=1, source_target_pairs={{0,15},{1,12},{2,13},{3,14},{4,3},{5,0},{6,1},{7,2},{8,7},{9,4},{1... | collective-permute-start | bytes 829448 | tf_op jit(solution)/shard_map/ppermute | solution.py:265
  79.5 5.2 %collective-permute-start.6 = (bf16[1080,128]{1,0:T(8,128)(2,1)}, bf16[1080,128]{1,0:T(8,128)(2,1)S(1)}, u32[]{:S(2)}, u32[]{:S(2)}) collective-permute-start(bf16[1080,128]{1,0:T(8,128)(2,1)} %get-tuple-element.34), channel_id=1, source_target_pairs={{0,7},{1,4},{2,5},{3,6},{4,11},{5,8},{6,9},{7,10},{8,15},{9,12},{1... | collective-permute-start | bytes 829448 | tf_op jit(solution)/shard_map/ppermute | solution.py:265
  84.8 0.9 collective-permute-start.7
  85.7 13.1 %collective-permute-done.3.refs_5_ = bf16[1080,128]{1,0:T(8,128)(2,1)S(1)} collective-permute-done((bf16[1080,128]{1,0:T(8,128)(2,1)}, bf16[1080,128]{1,0:T(8,128)(2,1)S(1)}, u32[]{:S(2)}, u32[]{:S(2)}) %collective-permute-start.3) | collective-permute-done | bytes 276512 | tf_op jit(solution)/shard_map/ppermute | solution.py:265
  98.8 3.7 %collective-permute-start.8 = (bf16[1080,128]{1,0:T(8,128)(2,1)}, bf16[1080,128]{1,0:T(8,128)(2,1)}, u32[]{:S(2)}, u32[]{:S(2)}) collective-permute-start(bf16[1080,128]{1,0:T(8,128)(2,1)} %get-tuple-element.36), channel_id=1, source_target_pairs={{0,2},{1,3},{2,0},{3,1},{4,6},{5,7},{6,4},{7,5},{8,10},{9,11},{10,... | collective-permute-start | bytes 829448 | tf_op jit(solution)/shard_map/ppermute | solution.py:265
  102.5 2.1 %collective-permute-start.9 = (bf16[1080,128]{1,0:T(8,128)(2,1)}, bf16[1080,128]{1,0:T(8,128)(2,1)}, u32[]{:S(2)}, u32[]{:S(2)}) collective-permute-start(bf16[1080,128]{1,0:T(8,128)(2,1)} %get-tuple-element.37), channel_id=1, source_target_pairs={{0,8},{1,9},{2,10},{3,11},{4,12},{5,13},{6,14},{7,15},{8,0},{9,1},... | collective-permute-start | bytes 829448 | tf_op jit(solution)/shard_map/ppermute | solution.py:265
  104.6 0.9 copy-done.2
  105.5 0.8 rolled.1
  106.4 3.2 %collective-permute-done.8.refs_10_ = bf16[1080,128]{1,0:T(8,128)(2,1)} collective-permute-done((bf16[1080,128]{1,0:T(8,128)(2,1)}, bf16[1080,128]{1,0:T(8,128)(2,1)}, u32[]{:S(2)}, u32[]{:S(2)}) %collective-permute-start.8) | collective-permute-done | bytes 276512 | tf_op jit(solution)/shard_map/ppermute | solution.py:265
  109.6 3.0 %collective-permute-done.9.refs_11_ = bf16[1080,128]{1,0:T(8,128)(2,1)} collective-permute-done((bf16[1080,128]{1,0:T(8,128)(2,1)}, bf16[1080,128]{1,0:T(8,128)(2,1)}, u32[]{:S(2)}, u32[]{:S(2)}) %collective-permute-start.9) | collective-permute-done | bytes 276512 | tf_op jit(solution)/shard_map/ppermute | solution.py:265
  112.6 1.0 copy-done
  113.6 6.8 %decode.1 = (bf16[4,88,2048]{2,1,0:T(8,128)(2,1)}, bf16[4,88,2048]{2,1,0:T(8,128)(2,1)}, bf16[4,88,2048]{2,1,0:T(8,128)(2,1)}, f32[12,128]{1,0:T(8,128)S(1)}) custom-call(s32[1]{0:T(128)} %bitcast.refs_0_, bf16[1080,128]{1,0:T(8,128)(2,1)S(1)} %copy-done, bf16[1080,128]{1,0:T(8,128)(2,1)S(1)} %collective-permute-done.refs_2_, ...), custom_call_target="tpu_custom_call" | custom-call | tf_op jit(solution)/shard_map/decode/pallas_call | solution.py:213
  120.4 0.6 fusion.1
  (22 shorter events, 0.5 us)
Async XLA Ops:
  15.8 1.4 %collective-permute-start.15 = (bf16[4,2048]{1,0:T(4,128)(2,1)S(1)}, bf16[4,2048]{1,0:T(4,128)(2,1)S(1)}, u32[]{:S(2)}, u32[]{:S(2)}) collective-permute-start(bf16[4,2048]{1,0:T(4,128)(2,1)S(1)} %bitcast.10), channel_id=1, source_target_pairs={{16,0},{32,16},{48,32},{64,48},{80,64},{96,80},{112,96},{128,112},... | collective-permute-start | bytes 49160 | tf_op jit(solution)/shard_map/ppermute | solution.py:251
  17.2 5.2 %collective-permute-start.16 = (bf16[8,2048]{1,0:T(8,128)(2,1)S(1)}, bf16[8,2048]{1,0:T(8,128)(2,1)S(1)}, u32[]{:S(2)}, u32[]{:S(2)}) collective-permute-start(bf16[8,2048]{1,0:T(8,128)(2,1)S(1)} %pad_maximum_fusion.2), channel_id=1, source_target_pairs={{32,0},{48,16},{64,32},{80,48},{96,64},{112,80},{128,96},{144,112}... | collective-permute-start | bytes 98312 | tf_op jit(solution)/shard_map/ppermute | solution.py:251
  22.5 7.0 %collective-permute-start.17 = (bf16[16,2048]{1,0:T(8,128)(2,1)S(1)}, bf16[16,2048]{1,0:T(8,128)(2,1)S(1)}, u32[]{:S(2)}, u32[]{:S(2)}) collective-permute-start(bf16[16,2048]{1,0:T(8,128)(2,1)S(1)} %pad_maximum_fusion.1), channel_id=1, source_target_pairs={{64,0},{80,16},{96,32},{112,48},{128,64},{144,80},{160,96},{176,11... | collective-permute-start | bytes 196616 | tf_op jit(solution)/shard_map/ppermute | solution.py:251
  29.4 15.3 %collective-permute-start.18 = (bf16[32,2048]{1,0:T(8,128)(2,1)S(1)}, bf16[32,2048]{1,0:T(8,128)(2,1)S(1)}, u32[]{:S(2)}, u32[]{:S(2)}) collective-permute-start(bf16[32,2048]{1,0:T(8,128)(2,1)S(1)} %pad_maximum_fusion), channel_id=1, source_target_pairs={{128,0},{144,16},{160,32},{176,48},{192,64},{208,80},{224,96},{240... | collective-permute-start | bytes 393224 | tf_op jit(solution)/shard_map/ppermute | solution.py:251
  39.1 16.3 %collective-permute-start = (bf16[1080,128]{1,0:T(8,128)(2,1)}, bf16[1080,128]{1,0:T(8,128)(2,1)S(1)}, u32[]{:S(2)}, u32[]{:S(2)}) collective-permute-start(bf16[1080,128]{1,0:T(8,128)(2,1)} %get-tuple-element.28), channel_id=1, source_target_pairs={{0,1},{1,2},{2,3},{3,0},{4,5},{5,6},{6,7},{7,4},{8,9},{9,10},{10,1... | collective-permute-start | bytes 829448 | tf_op jit(solution)/shard_map/ppermute | solution.py:265
  39.8 18.8 %collective-permute-start.1 = (bf16[1080,128]{1,0:T(8,128)(2,1)}, bf16[1080,128]{1,0:T(8,128)(2,1)S(1)}, u32[]{:S(2)}, u32[]{:S(2)}) collective-permute-start(bf16[1080,128]{1,0:T(8,128)(2,1)} %get-tuple-element.29), channel_id=1, source_target_pairs={{0,3},{1,0},{2,1},{3,2},{4,7},{5,4},{6,5},{7,6},{8,11},{9,8},{10,9... | collective-permute-start | bytes 829448 | tf_op jit(solution)/shard_map/ppermute | solution.py:265
  42.4 16.2 %collective-permute-start.10 = (bf16[1080,128]{1,0:T(8,128)(2,1)}, bf16[1080,128]{1,0:T(8,128)(2,1)S(1)}, u32[]{:S(2)}, u32[]{:S(2)}) collective-permute-start(bf16[1080,128]{1,0:T(8,128)(2,1)} %get-tuple-element.38), channel_id=1, source_target_pairs={{0,6},{1,7},{2,4},{3,5},{4,10},{5,11},{6,8},{7,9},{8,14},{9,15},{1... | collective-permute-start | bytes 829448 | tf_op jit(solution)/shard_map/ppermute | solution.py:265
  42.4 20.2 %collective-permute-start.11 = (bf16[1080,128]{1,0:T(8,128)(2,1)}, bf16[1080,128]{1,0:T(8,128)(2,1)S(1)}, u32[]{:S(2)}, u32[]{:S(2)}) collective-permute-start(bf16[1080,128]{1,0:T(8,128)(2,1)} %get-tuple-element.39), channel_id=1, source_target_pairs={{0,9},{1,10},{2,11},{3,8},{4,13},{5,14},{6,15},{7,12},{8,1},{9,2},... | collective-permute-start | bytes 829448 | tf_op jit(solution)/shard_map/ppermute | solution.py:265
  44.8 0.7 copy-start.1
  45.4 28.7 %collective-permute-start.12 = (bf16[1080,128]{1,0:T(8,128)(2,1)}, bf16[1080,128]{1,0:T(8,128)(2,1)S(1)}, u32[]{:S(2)}, u32[]{:S(2)}) collective-permute-start(bf16[1080,128]{1,0:T(8,128)(2,1)} %get-tuple-element.40), channel_id=1, source_target_pairs={{0,14},{1,15},{2,12},{3,13},{4,2},{5,3},{6,0},{7,1},{8,6},{9,7},{1... | collective-permute-start | bytes 829448 | tf_op jit(solution)/shard_map/ppermute | solution.py:265
  55.4 18.7 %collective-permute-start.13 = (bf16[1080,128]{1,0:T(8,128)(2,1)}, bf16[1080,128]{1,0:T(8,128)(2,1)S(1)}, u32[]{:S(2)}, u32[]{:S(2)}) collective-permute-start(bf16[1080,128]{1,0:T(8,128)(2,1)} %get-tuple-element.41), channel_id=1, source_target_pairs={{0,11},{1,8},{2,9},{3,10},{4,15},{5,12},{6,13},{7,14},{8,3},{9,0},... | collective-permute-start | bytes 829448 | tf_op jit(solution)/shard_map/ppermute | solution.py:265
  58.6 20.9 %collective-permute-start.14 = (bf16[1080,128]{1,0:T(8,128)(2,1)}, bf16[1080,128]{1,0:T(8,128)(2,1)S(1)}, u32[]{:S(2)}, u32[]{:S(2)}) collective-permute-start(bf16[1080,128]{1,0:T(8,128)(2,1)} %get-tuple-element.42), channel_id=1, source_target_pairs={{0,10},{1,11},{2,8},{3,9},{4,14},{5,15},{6,12},{7,13},{8,2},{9,3},... | collective-permute-start | bytes 829448 | tf_op jit(solution)/shard_map/ppermute | solution.py:265
  58.6 26.2 %collective-permute-start.2 = (bf16[1080,128]{1,0:T(8,128)(2,1)}, bf16[1080,128]{1,0:T(8,128)(2,1)S(1)}, u32[]{:S(2)}, u32[]{:S(2)}) collective-permute-start(bf16[1080,128]{1,0:T(8,128)(2,1)} %get-tuple-element.30), channel_id=1, source_target_pairs={{0,4},{1,5},{2,6},{3,7},{4,8},{5,9},{6,10},{7,11},{8,12},{9,13},{1... | collective-permute-start | bytes 829448 | tf_op jit(solution)/shard_map/ppermute | solution.py:265
  62.6 36.2 %collective-permute-start.3 = (bf16[1080,128]{1,0:T(8,128)(2,1)}, bf16[1080,128]{1,0:T(8,128)(2,1)S(1)}, u32[]{:S(2)}, u32[]{:S(2)}) collective-permute-start(bf16[1080,128]{1,0:T(8,128)(2,1)} %get-tuple-element.31), channel_id=1, source_target_pairs={{0,12},{1,13},{2,14},{3,15},{4,0},{5,1},{6,2},{7,3},{8,4},{9,5},{1... | collective-permute-start | bytes 829448 | tf_op jit(solution)/shard_map/ppermute | solution.py:265
  74.1 28.4 %collective-permute-start.4 = (bf16[1080,128]{1,0:T(8,128)(2,1)}, bf16[1080,128]{1,0:T(8,128)(2,1)S(1)}, u32[]{:S(2)}, u32[]{:S(2)}) collective-permute-start(bf16[1080,128]{1,0:T(8,128)(2,1)} %get-tuple-element.32), channel_id=1, source_target_pairs={{0,5},{1,6},{2,7},{3,4},{4,9},{5,10},{6,11},{7,8},{8,13},{9,14},{1... | collective-permute-start | bytes 829448 | tf_op jit(solution)/shard_map/ppermute | solution.py:265
  74.1 32.2 %collective-permute-start.5 = (bf16[1080,128]{1,0:T(8,128)(2,1)}, bf16[1080,128]{1,0:T(8,128)(2,1)S(1)}, u32[]{:S(2)}, u32[]{:S(2)}) collective-permute-start(bf16[1080,128]{1,0:T(8,128)(2,1)} %get-tuple-element.33), channel_id=1, source_target_pairs={{0,15},{1,12},{2,13},{3,14},{4,3},{5,0},{6,1},{7,2},{8,7},{9,4},{1... | collective-permute-start | bytes 829448 | tf_op jit(solution)/shard_map/ppermute | solution.py:265
  79.5 26.9 %collective-permute-start.6 = (bf16[1080,128]{1,0:T(8,128)(2,1)}, bf16[1080,128]{1,0:T(8,128)(2,1)S(1)}, u32[]{:S(2)}, u32[]{:S(2)}) collective-permute-start(bf16[1080,128]{1,0:T(8,128)(2,1)} %get-tuple-element.34), channel_id=1, source_target_pairs={{0,7},{1,4},{2,5},{3,6},{4,11},{5,8},{6,9},{7,10},{8,15},{9,12},{1... | collective-permute-start | bytes 829448 | tf_op jit(solution)/shard_map/ppermute | solution.py:265
  84.8 21.6 %collective-permute-start.7 = (bf16[1080,128]{1,0:T(8,128)(2,1)}, bf16[1080,128]{1,0:T(8,128)(2,1)}, u32[]{:S(2)}, u32[]{:S(2)}) collective-permute-start(bf16[1080,128]{1,0:T(8,128)(2,1)} %get-tuple-element.35), channel_id=1, source_target_pairs={{0,13},{1,14},{2,15},{3,12},{4,1},{5,2},{6,3},{7,0},{8,5},{9,6},{1... | collective-permute-start | bytes 829448 | tf_op jit(solution)/shard_map/ppermute | solution.py:265
  98.8 10.8 %collective-permute-start.8 = (bf16[1080,128]{1,0:T(8,128)(2,1)}, bf16[1080,128]{1,0:T(8,128)(2,1)}, u32[]{:S(2)}, u32[]{:S(2)}) collective-permute-start(bf16[1080,128]{1,0:T(8,128)(2,1)} %get-tuple-element.36), channel_id=1, source_target_pairs={{0,2},{1,3},{2,0},{3,1},{4,6},{5,7},{6,4},{7,5},{8,10},{9,11},{10,... | collective-permute-start | bytes 829448 | tf_op jit(solution)/shard_map/ppermute | solution.py:265
  102.5 10.1 %collective-permute-start.9 = (bf16[1080,128]{1,0:T(8,128)(2,1)}, bf16[1080,128]{1,0:T(8,128)(2,1)}, u32[]{:S(2)}, u32[]{:S(2)}) collective-permute-start(bf16[1080,128]{1,0:T(8,128)(2,1)} %get-tuple-element.37), channel_id=1, source_target_pairs={{0,8},{1,9},{2,10},{3,11},{4,12},{5,13},{6,14},{7,15},{8,0},{9,1},... | collective-permute-start | bytes 829448 | tf_op jit(solution)/shard_map/ppermute | solution.py:265
  104.6 0.9 copy-start.2
  112.6 1.0 copy-start
